TPU v7x, 128 devices: a whole 4x4x4 slice. The times are simulated.
128 devices in a mesh: rep: 2 (over core), dp: 64 (over x, y, z).
Axes of the slice: x: 4, y: 4, z: 4, core: 2. Of those that a mesh axis runs over, the one named last changes fastest.
Arguments:
- x: bfloat16 [128, 2048, 1024], P(('rep', 'dp')), parts along dimension 0
- dy: bfloat16 [128, 2048, 1024], P(('rep', 'dp')), parts along dimension 0
- w_gate: bfloat16 [2, 1024, 3200], replicated
- w_up: bfloat16 [2, 1024, 3200], replicated
- w_down: bfloat16 [2, 3200, 1024], replicated
- m_w_gate: float32 [2, 1024, 3200], P(None, 'dp')
- m_w_up: float32 [2, 1024, 3200], P(None, 'dp')
- m_w_down: float32 [2, 3200, 1024], P(None, 'dp')
- v_w_gate: float32 [2, 1024, 3200], P(None, 'dp')
- v_w_up: float32 [2, 1024, 3200], P(None, 'dp')
- v_w_down: float32 [2, 3200, 1024], P(None, 'dp')
Outputs:
- output 1: bfloat16 [4, 1024, 3200], P('rep'), parts along dimension 0
- output 2: bfloat16 [4, 1024, 3200], P('rep'), parts along dimension 0
- output 3: bfloat16 [4, 3200, 1024], P('rep'), parts along dimension 0
- output 4: float32 [4, 1024, 3200], P('rep', 'dp'), parts along dimension 0
- output 5: float32 [4, 1024, 3200], P('rep', 'dp'), parts along dimension 0
- output 6: float32 [4, 3200, 1024], P('rep', 'dp'), parts along dimension 0
- output 7: float32 [4, 1024, 3200], P('rep', 'dp'), parts along dimension 0
- output 8: float32 [4, 1024, 3200], P('rep', 'dp'), parts along dimension 0
- output 9: float32 [4, 3200, 1024], P('rep', 'dp'), parts along dimension 0
There are 2 independent parts. A program takes and returns all parts, laid end to end along the dimension named above; an argument that names none is the same for every part.
All inputs are finite; a program needn't handle non-finite values.
Results may differ from a plain program's by a relative error of at most 0.022.
Values are sent between devices in bfloat16 or wider.
A program may use at most 1.5 GiB of HBM per device.

v0:
```python
import jax
import jax.numpy as jnp
from jax import lax

NAMES = ("w_gate", "w_up", "w_down")


def matmul(a, w):
    return jnp.dot(a, w, preferred_element_type=jnp.float32).astype(jnp.bfloat16)


def normed(h):
    wide = h.astype(jnp.float32)
    scale = lax.rsqrt(jnp.mean(wide**2, -1, keepdims=True) + 1e-6)
    return (wide * scale).astype(jnp.bfloat16)


def layer(h, w):
    a = normed(h)
    gate = jnp.dot(a, w["w_gate"], preferred_element_type=jnp.float32)
    up = jnp.dot(a, w["w_up"], preferred_element_type=jnp.float32)
    return h + matmul((jax.nn.silu(gate) * up).astype(jnp.bfloat16), w["w_down"])


def adamw(w, m, v, g):
    m = 0.9 * m + 0.1 * g
    v = 0.95 * v + 0.05 * g * g
    step = m * lax.rsqrt(v + 1e-8) + 0.1 * w
    return (w - 0.02 * step).astype(jnp.bfloat16), m, v


def stack(weights, h):
    for number in range(weights["w_gate"].shape[0]):
        h = layer(h, {name: w[number] for name, w in weights.items()})
    return h


def solution(mesh):
    groups = mesh.shape["rep"]

    def step(x, dy, *arrays):
        weights, m, v = (arrays[i : i + 3] for i in (0, 3, 6))
        x, dy = (t.reshape(groups, -1, *t.shape[1:]) for t in (x, dy))

        def of_a_group(x, dy):
            _, back = jax.vjp(lambda w: stack(w, x), dict(zip(NAMES, weights, strict=True)))
            by_weights = back(dy)[0]
            gradients = [by_weights[name].astype(jnp.float32) for name in NAMES]
            new = [adamw(w.astype(jnp.float32), m, v, g) for w, m, v, g in zip(weights, m, v, gradients, strict=True)]
            return tuple(one[which] for which in range(3) for one in new)

        return tuple(t.reshape(-1, *t.shape[2:]) for t in jax.vmap(of_a_group)(x, dy))

    return step
```

profile of v0, /device:TPU:0, one launch (start us, length us, event | category | flops | bytes accessed | tf_op | source)
XLA Modules:
  0.0 2102.8 jit_solution(15821852535628031266)
XLA Ops:
  10.3 6.6 copy.6
  17.0 22.0 %fusion.69 = f32[2048,3200]{1,0:T(8,128)} fusion(bf16[2,1024,3200]{2,1,0:T(8,128)(2,1)} %param, bf16[1,2048,1024]{2,1,0:T(8,128)(2,1)} %param.2, f32[2048]{0:T(1024)S(1)} %add_rsqrt_fusion), kind=kOutput, calls=%fused_computation.79 | convolution fusion | flops 13428064256 | bytes 36970496 | tf_op jit(solution)/vmap(jvp())/dot_general | solution.py:20
  39.0 18.0 fusion.67
  57.0 22.9 %fusion.28 = bf16[2048,3200]{1,0:T(8,128)(2,1)} fusion(f32[2048,3200]{1,0:T(8,128)} %fusion.67, f32[2048,3200]{1,0:T(8,128)} %fusion.69), kind=kLoop, calls=%fused_computation.41 | loop fusion | flops 39321600 | bytes 65536000
  79.9 22.2 %fusion.53 = (f32[2048]{0:T(1024)S(1)}, bf16[1,1,2048,1024]{2,3,1,0:T(8,128)(2,1)}) fusion(bf16[2048,3200]{1,0:T(8,128)(2,1)} %fusion.28, bf16[2,3200,1024]{2,1,0:T(8,128)(2,1)} %param.4, bf16[1,2048,1024]{1,2,0:T(8,128)(2,1)} %copy.6), kind=kOutput, calls=%fused_computation.62 | convolution fusion | flops 13432256512 | bytes 28057600 | tf_op jit(solution)/vmap(jvp())/dot_general | solution.py:9
  102.7 23.7 %fusion.58 = f32[2048,3200]{1,0:T(8,128)} fusion(bf16[2,1024,3200]{2,1,0:T(8,128)(2,1)} %param, bf16[1,1,2048,1024]{2,3,1,0:T(8,128)(2,1)} %get-tuple-element.46, f32[2048]{0:T(1024)S(1)} %bitcast.357), kind=kOutput, calls=%fused_computation.68 | convolution fusion | flops 13428064256 | bytes 36970496 | tf_op jit(solution)/vmap(jvp())/dot_general | solution.py:20
  126.4 20.9 fusion.61
  147.3 19.7 convolution_convert_fusion.1
  166.9 26.9 %fusion.8 = bf16[2048,3200]{1,0:T(8,128)(2,1)} fusion(f32[2048,3200]{1,0:T(8,128)} %fusion.58, f32[2048,3200]{1,0:T(8,128)} %fusion.61, bf16[2048,3200]{1,0:T(8,128)(2,1)} %convolution_convert_fusion.1), kind=kLoop, calls=%fused_computation.11 | loop fusion | flops 78643200 | bytes 78643200
  193.8 21.9 %convolution_bitcast_fusion = f32[1,1024,3200]{2,1,0:T(8,128)} fusion(bf16[2048,3200]{1,0:T(8,128)(2,1)} %fusion.8, bf16[1,1,2048,1024]{2,3,1,0:T(8,128)(2,1)} %get-tuple-element.46, f32[2048]{0:T(1024)S(1)} %bitcast.359), kind=kOutput, calls=%fused_computation.55 | convolution fusion | flops 13428064256 | bytes 30416896 | tf_op jit(solution)/vmap(transpose(jvp()))/dot_general | solution.py:20
  215.8 6.7 copy.7
  222.5 22.4 %fusion.26 = bf16[2048,1024]{0,1:T(8,128)(2,1)} fusion(bf16[2048,3200]{1,0:T(8,128)(2,1)} %convolution_convert_fusion.1, f32[2048,3200]{1,0:T(8,128)} %fusion.58, bf16[2,1024,3200]{2,1,0:T(8,128)(2,1)} %param.3), kind=kOutput, calls=%fused_computation.34 | convolution fusion | flops 13461094400 | bytes 50069504 | tf_op jit(solution)/vmap(transpose(jvp()))/dot_general | solution.py:21
  245.0 22.8 %fusion.55 = (f32[2048]{0:T(1024)S(1)}, bf16[2048,1024]{0,1:T(8,128)(2,1)}) fusion(bf16[1,1,2048,1024]{2,3,1,0:T(8,128)(2,1)} %get-tuple-element.46, bf16[2048,1024]{0,1:T(8,128)(2,1)} %fusion.26, bf16[2048,3200]{1,0:T(8,128)(2,1)} %fusion.8, bf16[2,1024,3200]{2,1,0:T(8,128)(2,1)} %param), kind=kOutput, calls=%fused_computation.64 | convolution fusion | flops 13432256512 | bytes 32251904 | tf_op jit(solution)/vmap(transpose(jvp()))/dot_general | solution.py:20
  267.8 6.7 fusion.83
  274.6 21.4 %convolution_convert_fusion = bf16[2048,3200]{1,0:T(8,128)(2,1)} fusion(bf16[2048,1024]{0,1:T(8,128)(2,1)} %fusion.83, bf16[2,3200,1024]{2,1,0:T(8,128)(2,1)} %param.4), kind=kOutput, calls=%fused_computation.35 | convolution fusion | flops 13428326400 | bytes 23855104 | tf_op jit(solution)/vmap(transpose(jvp()))/dot_general | solution.py:9
  296.0 32.0 %fusion.46 = f32[1,1024,3200]{2,1,0:T(8,128)} fusion(f32[2048,3200]{1,0:T(8,128)} %fusion.69, f32[2048,3200]{1,0:T(8,128)} %fusion.67, bf16[2048,3200]{1,0:T(8,128)(2,1)} %convolution_convert_fusion, bf16[1,2048,1024]{1,2,0:T(8,128)(2,1)S(1)} %copy-done.5, f32[2048]{0:T(1024)S(1)} %copy-done.18), kind=kOutput, calls=%fused_computation.56 | convolution fusion | flops 13500153856 | bytes 82845696 | tf_op jit(solution)/vmap(transpose(jvp()))/dot_general | solution.py:20
  328.1 26.0 %fusion.40 = f32[1,1024,3200]{2,1,0:T(8,128)} fusion(bf16[2048,3200]{1,0:T(8,128)(2,1)} %convolution_convert_fusion.1, f32[2048,3200]{1,0:T(8,128)} %fusion.58, bf16[1,1,2048,1024]{2,3,1,0:T(8,128)(2,1)} %get-tuple-element.46, f32[2048]{0:T(1024)S(1)} %bitcast.361), kind=kOutput, calls=%fused_computation.53 | convolution fusion | flops 13467385856 | bytes 56631296 | tf_op jit(solution)/vmap(transpose(jvp()))/dot_general | solution.py:21
  354.1 25.8 %fusion.43 = f32[1,1024,3200]{2,1,0:T(8,128)} fusion(bf16[2048,3200]{1,0:T(8,128)(2,1)} %convolution_convert_fusion, f32[2048,3200]{1,0:T(8,128)} %fusion.69, bf16[1,2048,1024]{1,2,0:T(8,128)(2,1)} %copy.6, f32[2048]{0:T(1024)S(1)} %copy-done.18), kind=kOutput, calls=%fused_computation.54 | convolution fusion | flops 13467385856 | bytes 56631296 | tf_op jit(solution)/vmap(transpose(jvp()))/dot_general | solution.py:21
  380.0 21.1 %convolution_bitcast_fusion.1 = f32[1,3200,1024]{2,1,0:T(8,128)} fusion(bf16[2048,3200]{1,0:T(8,128)(2,1)} %fusion.28, bf16[2048,1024]{0,1:T(8,128)(2,1)} %fusion.83), kind=kOutput, calls=%fused_computation.57 | convolution fusion | flops 13421772800 | bytes 30408704 | tf_op jit(solution)/vmap(transpose(jvp()))/dot_general | solution.py:9
  401.2 28.2 %fusion.37 = f32[1,3200,1024]{2,1,0:T(8,128)} fusion(f32[2048,3200]{1,0:T(8,128)} %fusion.61, f32[2048,3200]{1,0:T(8,128)} %fusion.58, bf16[1,2048,1024]{2,1,0:T(8,128)(2,1)} %param.5), kind=kOutput, calls=%fused_computation.52 | convolution fusion | flops 13461094400 | bytes 69730304 | tf_op jit(solution)/vmap(transpose(jvp()))/dot_general | solution.py:9
  429.4 556.4 %fusion.133 = (f32[56,1024]{1,0:T(8,128)S(1)}, f32[56,1024]{1,0:T(8,128)S(1)}) fusion(f32[1,3200,1024]{2,1,0:T(8,128)} %convolution_bitcast_fusion.1, f32[1,3200,1024]{2,1,0:T(8,128)} %fusion.37), kind=kCustom, calls=%all-reduce-scatter.2 | all-reduce-scatter fusion | flops 7340033 | bytes 26673664
  997.7 7.0 collective-permute-start
  1012.3 5.7 collective-permute-start.11
  1032.9 7.0 concatenate.1
  1046.8 367.0 %reduce-scatter.25.cloned.1.call-done = f32[1,16,3200]{2,1,0:T(8,128)} async-done(((f32[1,1024,3200]{2,1,0:T(8,128)}), f32[1,16,3200]{2,1,0:T(8,128)}) %reduce-scatter.25.cloned.1.call-update) | async-done | bytes 204816
  1414.7 379.5 %reduce-scatter.27.cloned.1.call-done = f32[1,16,3200]{2,1,0:T(8,128)} async-done(((f32[1,1024,3200]{2,1,0:T(8,128)}), f32[1,16,3200]{2,1,0:T(8,128)}) %reduce-scatter.27.cloned.1.call-update) | async-done | bytes 204816
  1799.6 85.3 %all-gather.14.cloned.1.call-done = bf16[1,2,3200,1024]{3,1,0,2:T(2,128)(2,1)} async-done(((bf16[1,2,50,1024]{3,1,0,2:T(2,128)(2,1)}), bf16[1,2,3200,1024]{3,1,0,2:T(2,128)(2,1)}) %all-gather.14.cloned.1.call-update) | async-done | bytes 13107216 | tf_op jit(solution)/reshape | solution.py:52
  1884.9 12.9 copy.11
  1897.8 83.1 %all-gather.10.cloned.1.call-done = bf16[1,2,1024,3200]{3,2,1,0:T(8,128)(2,1)} async-done(((bf16[1,2,16,3200]{3,2,1,0:T(8,128)(2,1)}), bf16[1,2,1024,3200]{3,2,1,0:T(8,128)(2,1)}) %all-gather.10.cloned.1.call-update) | async-done | bytes 13107216 | tf_op jit(solution)/reshape | solution.py:52
  1980.9 96.2 %all-gather.12.cloned.1.call-done = bf16[1,2,1024,3200]{3,2,1,0:T(8,128)(2,1)} async-done(((bf16[1,2,16,3200]{3,2,1,0:T(8,128)(2,1)}), bf16[1,2,1024,3200]{3,2,1,0:T(8,128)(2,1)}) %all-gather.12.cloned.1.call-update) | async-done | bytes 13107216 | tf_op jit(solution)/reshape | solution.py:52
  2077.1 11.4 copy.34
  2090.5 4.9 copy.35
  (114 shorter events, 52.0 us)
Async XLA Ops:
  7.2 1035.5 %reduce-scatter.21.cloned.1.call-start = ((), (), s32[]{:S(2)}) async-start(), calls=%async_computation.7 | async-start | bytes 13312000
  10.3 28.7 %slice-start = ((s8[13107200]{0:T(1024)(128)(4,1)}), s8[524288]{0:T(1024)(128)(4,1)S(1)}, s32[]{:S(2)}) async-start(s8[13107200]{0:T(1024)(128)(4,1)} %bitcast.363), calls=%async_computation.11 | async-start | bytes 1048576
  16.9 22.1 %copy-start.17 = (f32[2048]{0:T(1024)}, f32[2048]{0:T(1024)S(1)}, u32[]{:S(2)}) copy-start(f32[2048]{0:T(1024)S(1)} %add_rsqrt_fusion) | copy-start | bytes 24580
  16.9 22.1 %copy-start.1 = (bf16[1,2048,1024]{2,1,0:T(8,128)(2,1)S(1)}, bf16[1,2048,1024]{2,1,0:T(8,128)(2,1)}, u32[]{:S(2)}) copy-start(bf16[1,2048,1024]{2,1,0:T(8,128)(2,1)} %param.2) | copy-start | bytes 12582916
  16.9 22.0 %slice-start.1 = ((s8[13107200]{0:T(1024)(128)(4,1)}), s8[4194304]{0:T(1024)(128)(4,1)S(1)}, s32[]{:S(2)}) async-start(s8[13107200]{0:T(1024)(128)(4,1)} %bitcast.363), calls=%async_computation.12 | async-start | bytes 8388608
  102.7 23.7 %copy-start.3 = (bf16[1,1,2048,1024]{2,3,1,0:T(8,128)(2,1)S(1)}, bf16[1,1,2048,1024]{2,3,1,0:T(8,128)(2,1)}, u32[]{:S(2)}) copy-start(bf16[1,1,2048,1024]{2,3,1,0:T(8,128)(2,1)} %get-tuple-element.46) | copy-start | bytes 12582916
  215.8 827.9 %reduce-scatter.23.cloned.1.call-start = ((), (), s32[]{:S(2)}) async-start(), calls=%async_computation.8 | async-start | bytes 13312000
  245.0 22.8 %copy-start.16 = (f32[2048]{0:T(1024)S(1)}, f32[2048]{0:T(1024)}, u32[]{:S(2)}) copy-start(f32[2048]{0:T(1024)} %copy-done.15) | copy-start | bytes 24580
  245.0 22.9 %copy-start = (bf16[1,2048,1024]{1,2,0:T(8,128)(2,1)S(1)}, bf16[1,2048,1024]{1,2,0:T(8,128)(2,1)}, u32[]{:S(2)}) copy-start(bf16[1,2048,1024]{1,2,0:T(8,128)(2,1)} %copy.7) | copy-start | bytes 12582916
  328.0 1085.7 %reduce-scatter.25.cloned.1.call-start = ((), (), s32[]{:S(2)}) async-start(), calls=%async_computation.9 | async-start | bytes 13312000
  354.1 1440.1 %reduce-scatter.27.cloned.1.call-start = ((), (), s32[]{:S(2)}) async-start(), calls=%async_computation.10 | async-start | bytes 13312000
  380.0 1504.9 %all-gather.14.cloned.1.call-start = ((), (), s32[]{:S(2)}) async-start(), calls=%async_computation.6 | async-start | bytes 13312000 | tf_op jit(solution)/reshape | solution.py:52
  429.4 596.7 %copy-start.19 = (u32[128]{0:T(128)S(1)}, u32[128]{0:T(128)}, u32[]{:S(2)}) copy-start(u32[128]{0:T(128)} %constant.62) | copy-start | bytes 1540
  429.4 615.2 %copy-start.6 = (f32[2,16,3200]{2,1,0:T(8,128)S(1)}, f32[2,16,3200]{2,1,0:T(8,128)}, u32[]{:S(2)}) copy-start(f32[2,16,3200]{2,1,0:T(8,128)} %param.6) | copy-start | bytes 1228804
  429.4 615.2 %copy-start.7 = (f32[2,16,3200]{2,1,0:T(8,128)S(1)}, f32[2,16,3200]{2,1,0:T(8,128)}, u32[]{:S(2)}) copy-start(f32[2,16,3200]{2,1,0:T(8,128)} %param.1) | copy-start | bytes 1228804
  429.4 1365.8 %copy-start.8 = (f32[2,16,3200]{2,1,0:T(8,128)S(1)}, f32[2,16,3200]{2,1,0:T(8,128)}, u32[]{:S(2)}) copy-start(f32[2,16,3200]{2,1,0:T(8,128)} %param.8) | copy-start | bytes 1228804
  985.8 11.9 collective-permute-start.1
  987.1 17.6 collective-permute-start.2
  988.4 5.0 collective-permute-start.6
  989.8 5.0 collective-permute-start.13
  991.1 15.6 collective-permute-start.3
  993.4 15.2 collective-permute-start.4
  994.7 17.6 collective-permute-start.5
  997.7 20.4 collective-permute-start
  1004.7 16.8 collective-permute-start.8
  1006.6 25.5 %collective-permute-start.9 = (bf16[56,1024]{1,0:T(8,128)(2,1)S(1)}, bf16[56,1024]{1,0:T(8,128)(2,1)}, u32[]{:S(2)}, u32[]{:S(2)}) collective-permute-start(bf16[56,1024]{1,0:T(8,128)(2,1)S(1)} %convert.65), channel_id=1, source_target_pairs={{0,3},{1,4},{2,5},{3,6},{4,7},{5,8},{6,9},{7,10},{8,11},{9,12},{10... | collective-permute-start | bytes 344072
  1008.6 23.6 %collective-permute-start.10 = (bf16[56,1024]{1,0:T(8,128)(2,1)S(1)}, bf16[56,1024]{1,0:T(8,128)(2,1)}, u32[]{:S(2)}, u32[]{:S(2)}) collective-permute-start(bf16[56,1024]{1,0:T(8,128)(2,1)S(1)} %convert.65), channel_id=1, source_target_pairs={{0,4},{1,5},{2,6},{3,7},{4,8},{5,9},{6,10},{7,11},{8,12},{9,13},{1... | collective-permute-start | bytes 344072
  1012.3 19.9 collective-permute-start.11
  1018.0 14.2 collective-permute-start.12
  1021.5 11.4 collective-permute-start.7
  1042.6 938.3 %all-gather.10.cloned.1.call-start = ((), (), s32[]{:S(2)}) async-start(), calls=%async_computation.4 | async-start | bytes 13312000 | tf_op jit(solution)/reshape | solution.py:52
  1046.7 1030.4 %all-gather.12.cloned.1.call-start = ((), (), s32[]{:S(2)}) async-start(), calls=%async_computation.5 | async-start | bytes 13312000 | tf_op jit(solution)/reshape | solution.py:52
  (13 other events, 170.2 us)
Sparse Core Ops, SparseCore 0:
  215.9 399.4 reduce-scatter.20
  617.8 414.6 reduce-scatter.22
  1035.0 378.7 reduce-scatter.24
  1416.6 377.5 reduce-scatter.26
  1797.5 87.2 all-gather.13
  1888.2 92.6 all-gather.9
  1984.4 92.6 all-gather.11
where the time goes:
time: 2110 us; the launch traced here: 2100 us
  waiting for transfers between devices  1010 us (48%)
  blocking collectives  556 us (26%)
  matrix products  348 us (16%)
  other arithmetic  69.4 us (3%)
  local copies, waits for them, and re-layouts  60.8 us (3%)
  starting transfers between devices  39.3 us (2%)
    unnamed x25, waiting for transfers between devices  748 us
    unnamed x1, blocking collectives  556 us
    reshape x3, waiting for transfers between devices, step(): t.reshape(-1, *t.shape[2:])  265 us
    dot_general x5, matrix products, layer(): gate = jnp.dot(a, w['w_gate'], preferred_element_type=jnp.float32)  122 us
    dot_general x5, matrix products, layer(): up = jnp.dot(a, w['w_up'], preferred_element_type=jnp.float32)  113 us
    dot_general x5, matrix products, matmul(): jnp.dot(a, w, preferred_element_type=jnp.float32).astype(jnp.bfloat16)  113 us
    unnamed x60, local copies, waits for them, and re-layouts  59.8 us
    unnamed x6, other arithmetic  56.5 us
  transfers between devices with their start and end apart: 21, of which 6 were waited for; matrix products, arithmetic and copies ran while one was open for 38% of the time, Pallas kernels for 0%

commit v1 on v0

v1 whole, which is shorter than its diff:
```python
import functools

import jax
import jax.numpy as jnp
from jax import lax
from jax.experimental import pallas as pl
from jax.experimental.pallas import tpu as pltpu
from jax.sharding import PartitionSpec as P

NAMES = ("w_gate", "w_up", "w_down")
MESH = pl.DeviceIdType.MESH
BF, F32 = jnp.bfloat16, jnp.float32
TOKENS, D, FF = 2048, 1024, 3200
STRIDE = (16, 4, 1)
ORDER = ((1, 2, 0), (2, 0, 1), (0, 1, 2))
CUTS = ((0, 768), (768, 768), (1536, 768), (2304, 896))
CHUNKS = len(CUTS)
DOWN = D // CHUNKS


def mod4(v):
    return lax.rem(v + 8, 4)


class Net:
    def __init__(self, send_sems, recv_sems):
        self.me = lax.axis_index("dp")
        self.at = (lax.div(self.me, 16), lax.rem(lax.div(self.me, 4), 4), lax.rem(self.me, 4))
        self.send_sems, self.recv_sems = send_sems, recv_sems
        self.used = 0
        self.sent = []

    def device(self, dim, off):
        return self.me + (mod4(self.at[dim] + off) - self.at[dim]) * STRIDE[dim]

    def greet(self):
        barrier = pltpu.get_barrier_semaphore()
        for dim in range(3):
            for off in (1, 2, 3):
                pl.semaphore_signal(barrier, inc=1, device_id={"dp": self.device(dim, off)}, device_id_type=MESH)
        pl.semaphore_wait(barrier, 9)

    def send(self, src, dst, dim, off):
        n = self.used
        self.used += 1
        copy = pltpu.make_async_remote_copy(
            src_ref=src, dst_ref=dst, send_sem=self.send_sems.at[n], recv_sem=self.recv_sems.at[n],
            device_id={"dp": self.device(dim, off)}, device_id_type=MESH,
        )
        copy.start()
        self.sent.append(copy)
        return copy

    def finish(self):
        for copy in self.sent:
            copy.wait_send()
        self.sent = []


def slab(ref, axis, c):
    return ref.at[(slice(None),) * axis + (c,)]


def blocks(shape):
    lead, rows = shape[:-2], shape[-2]
    if rows == 200:
        inner = [(pl.ds(r, 40), slice(None)) for r in range(0, 200, 40)]
    else:
        inner = [(slice(None), slice(None))]
    if len(lead) == 2:
        return lead[0], lambda i: [(i, j) + tail for j in range(lead[1]) for tail in inner]
    if len(lead) == 1:
        return lead[0], lambda i: [(i,) + tail for tail in inner]
    return 1, lambda i: inner


def add_into(dst, *refs):
    trips, cover = blocks(dst.shape)

    def body(i, _):
        for where in cover(i):
            total = refs[0][where].astype(F32)
            for ref in refs[1:]:
                total = total + ref[where].astype(F32)
            dst[where] = total.astype(dst.dtype)
        return 0

    if trips == 1:
        body(0, 0)
    else:
        lax.fori_loop(0, trips, body, 0)


def scatter_buffers(which, width):
    if which < 2:
        g, a, b, c = (4, 4, 4, 16, width), (4, 4, 16, width), (4, 16, width), (16, width)
    else:
        g, a, b, c = (4, 4, 200, width), (4, 200, width), (200, width), (50, width)
    shapes = [g] + [a] * 3 + [b] * 3 + [c] * 3
    scratch = [pltpu.VMEM(s, BF) for s in shapes]
    if which == 2:
        scratch += [pltpu.VMEM((200, width), F32), pltpu.VMEM((4, 50, width), BF)]
    return scratch


SCATTER_SENDS = 9


class Scatter:
    def __init__(self, net, which, chunk, refs):
        self.net, self.which = net, which
        self.g, (self.a1, self.a2, self.a3), (self.b1, self.b2, self.b3), self.c = refs[0], refs[1:4], refs[4:7], refs[7:10]
        if which == 2:
            self.wide, self.cut = refs[10:12]
        self.dims = ORDER[which]
        self.axes = ((1, 1), (2, 0), (0, 0))[which]
        self.way = 1 if (chunk + which) % 2 == 0 else -1

    def start_a(self):
        dim, p, s = self.dims[0], self.net.at[self.dims[0]], self.way
        cut = lambda c: slab(self.g, self.axes[0], mod4(c))
        self.far = self.net.send(cut(p + 2), self.a1, dim, s)
        self.near = self.net.send(cut(p - s), self.a2, dim, -s)

    def mid_a(self):
        dim, p, s = self.dims[0], self.net.at[self.dims[0]], self.way
        self.far.wait_recv()
        add_into(self.a1, self.a1, slab(self.g, self.axes[0], mod4(p + s)))
        self.both = self.net.send(self.a1, self.a3, dim, s)

    def end_a(self):
        p = self.net.at[self.dims[0]]
        self.near.wait_recv()
        self.both.wait_recv()
        add_into(self.a2, self.a2, self.a3, slab(self.g, self.axes[0], p))
        dim, p, s = self.dims[1], self.net.at[self.dims[1]], self.way
        cut = lambda c: slab(self.a2, self.axes[1], mod4(c))
        self.far = self.net.send(cut(p + 2), self.b1, dim, s)
        self.near = self.net.send(cut(p - s), self.b2, dim, -s)

    def mid_b(self):
        dim, p, s = self.dims[1], self.net.at[self.dims[1]], self.way
        self.far.wait_recv()
        add_into(self.b1, self.b1, slab(self.a2, self.axes[1], mod4(p + s)))
        self.both = self.net.send(self.b1, self.b3, dim, s)

    def end_b(self):
        p = self.net.at[self.dims[1]]
        self.near.wait_recv()
        self.both.wait_recv()
        mine = slab(self.a2, self.axes[1], p)
        if self.which < 2:
            self.cut = self.b2
            add_into(self.b2, self.b2, self.b3, mine)
        else:
            add_into(self.wide, self.b2, self.b3, mine)
            for j in range(4):
                self.cut[j] = self.wide[50 * j : 50 * j + 50, :].astype(BF)
        dim, p = self.dims[2], self.net.at[self.dims[2]]
        self.last = [self.net.send(self.cut.at[mod4(p + off)], self.c[off - 1], dim, off) for off in (1, 2, 3)]

    def end_c(self):
        p = self.net.at[self.dims[2]]
        total = self.cut[p].astype(F32)
        for copy, ref in zip(self.last, self.c, strict=True):
            copy.wait_recv()
            total = total + ref[...].astype(F32)
        return total.astype(BF).astype(F32)


def adamw(w, m, v, g):
    m = 0.9 * m + 0.1 * g
    v = 0.95 * v + 0.05 * g * g
    step = m * lax.rsqrt(v + 1e-8) + 0.1 * w
    return (w - 0.02 * step).astype(BF), m, v


GATHER_SENDS = 9


class Gather:
    def __init__(self, net, which, chunk, out, small=None, wide=None):
        self.net, self.which, self.out, self.small, self.wide = net, which, out, small, wide
        self.dims = ORDER[which][::-1]
        self.way = 1 if (chunk + which) % 2 == 0 else -1

    def view(self, fixed):
        dims = (0, 1, 2) if self.which < 2 else (0, 1)
        where = [fixed.get(d, slice(None)) for d in dims]
        while where and isinstance(where[-1], slice):
            where.pop()
        return self.out.at[tuple(where)] if where else self.out

    def start(self, mine):
        x, y, z = self.net.at
        if self.which < 2:
            block = self.view({0: x, 1: y, 2: z})
        else:
            block = self.small.at[z]
        block[...] = mine
        self.first = [self.net.send(block, block, self.dims[0], off) for off in (1, 2, 3)]

    def _both(self, fixed, dim):
        part = self.view(fixed)
        return [self.net.send(part, part, dim, off) for off in (self.way, -self.way)]

    def _on(self, fixed, dim):
        part = self.view({**fixed, dim: mod4(self.net.at[dim] - self.way)})
        return self.net.send(part, part, dim, self.way)

    def second(self):
        for copy in self.first:
            copy.wait_recv()
        at = self.net.at
        a, b, c = ORDER[self.which]
        if self.which == 2:
            for j in range(4):
                self.wide[50 * j : 50 * j + 50, :] = self.small[j].astype(F32)
            row = self.view({0: at[0], 1: at[1]})
            row[...] = self.wide[...].astype(BF)
        self.pair = self._both({a: at[a], b: at[b]}, b)

    def second_on(self):
        at = self.net.at
        a, b, _ = ORDER[self.which]
        self.pair[0].wait_recv()
        self.pair[1].wait_recv()
        self.passed = self._on({a: at[a]}, b)

    def third(self):
        at = self.net.at
        a = ORDER[self.which][0]
        self.passed.wait_recv()
        self.pair = self._both({a: at[a]}, a)

    def third_on(self):
        a = ORDER[self.which][0]
        self.pair[0].wait_recv()
        self.pair[1].wait_recv()
        self.passed = self._on({}, a)

    def last(self):
        self.passed.wait_recv()


def ticks(stages):
    return [(s, t - s) for t in range(CHUNKS + stages - 1) for s in range(stages) if 0 <= t - s < CHUNKS]


def width(which, chunk):
    return CUTS[chunk][1] if which < 2 else DOWN


def columns(which, chunk):
    return pl.ds(*CUTS[chunk]) if which < 2 else pl.ds(DOWN * chunk, DOWN)


def split(refs, counts):
    out, at = [], 0
    for n in counts:
        out.append(refs[at : at + n])
        at += n
    return out


SCATTER_REFS = (10, 10, 12)


def scatter_kernel(*refs):
    grads, ws, ms, vs, w_out, m_out, v_out, rest = split(refs, (3, 3, 3, 3, 3, 3, 3, len(refs) - 21))
    send_sems, recv_sems, load_sems = rest[-3:]
    parts = split(rest[:-3], SCATTER_REFS * CHUNKS)
    net = Net(send_sems, recv_sems)
    net.greet()
    units = [[Scatter(net, which, k, parts[3 * k + which]) for which in range(3)] for k in range(CHUNKS)]
    loads = [
        [
            pltpu.make_async_copy(grads[which].at[..., columns(which, k)], units[k][which].g, load_sems.at[3 * k + which])
            for which in range(3)
        ]
        for k in range(CHUNKS)
    ]
    for chunk in loads:
        for copy in chunk:
            copy.start()
    for stage, k in ticks(6):
        for which in range(3):
            unit = units[k][which]
            if stage == 0:
                loads[k][which].wait()
                unit.start_a()
            elif stage < 5:
                (unit.mid_a, unit.end_a, unit.mid_b, unit.end_b)[stage - 1]()
            else:
                cols = columns(which, k)
                w, m, v = adamw(ws[which][:, cols].astype(F32), ms[which][:, cols], vs[which][:, cols], unit.end_c())
                w_out[which][:, cols] = w
                m_out[which][:, cols] = m
                v_out[which][:, cols] = v
    net.finish()


def scatter_step(grads, w, m, v, ident):
    small = [(16, FF), (16, FF), (50, D)]
    n = SCATTER_SENDS * 3 * CHUNKS
    scratch = [s for k in range(CHUNKS) for which in range(3) for s in scatter_buffers(which, width(which, k))]
    vmem = pl.BlockSpec(memory_space=pltpu.VMEM)
    out = pl.pallas_call(
        scatter_kernel,
        out_shape=[jax.ShapeDtypeStruct(s, t) for t in (BF, F32, F32) for s in small],
        in_specs=[pl.BlockSpec(memory_space=pl.ANY)] * 3 + [vmem] * 9,
        out_specs=[vmem] * 9,
        scratch_shapes=scratch
        + [pltpu.SemaphoreType.DMA((n,)), pltpu.SemaphoreType.DMA((n,)), pltpu.SemaphoreType.DMA((3 * CHUNKS,))],
        compiler_params=pltpu.CompilerParams(collective_id=ident, has_side_effects=True, vmem_limit_bytes=60 * 2**20),
        name=f"scatter_{ident}",
    )(*grads, *w, *m, *v)
    return out[:3], out[3:6], out[6:]


def gather_buffers(which, width):
    if which < 2:
        return [pltpu.VMEM((4, 4, 4, 16, width), BF)]
    return [pltpu.VMEM((4, 4, 200, width), BF), pltpu.VMEM((4, 50, width), BF), pltpu.VMEM((200, width), F32)]


def gather_kernel(*refs):
    ws, outs, rest = split(refs, (3, 3, len(refs) - 6))
    send_sems, recv_sems, store_sems = rest[-3:]
    parts = split(rest[:-3], (1, 1, 3) * CHUNKS)
    net = Net(send_sems, recv_sems)
    net.greet()
    units = [[Gather(net, which, k, *parts[3 * k + which]) for which in range(3)] for k in range(CHUNKS)]
    stores = []
    for stage, k in ticks(6):
        for which in range(3):
            unit = units[k][which]
            if stage == 0:
                unit.start(ws[which][:, columns(which, k)])
            else:
                (unit.second, unit.second_on, unit.third, unit.third_on, unit.last)[stage - 1]()
            if stage == 5:
                copy = pltpu.make_async_copy(unit.out, outs[which].at[..., columns(which, k)], store_sems.at[3 * k + which])
                copy.start()
                stores.append(copy)
    for copy in stores:
        copy.wait()
    net.finish()


def gather_step(w, ident):
    n = GATHER_SENDS * 3 * CHUNKS
    scratch = [s for k in range(CHUNKS) for which in range(3) for s in gather_buffers(which, width(which, k))]
    return pl.pallas_call(
        gather_kernel,
        out_shape=[jax.ShapeDtypeStruct(s, BF) for s in [(4, 4, 4, 16, FF)] * 2 + [(4, 4, 200, D)]],
        in_specs=[pl.BlockSpec(memory_space=pltpu.VMEM)] * 3,
        out_specs=[pl.BlockSpec(memory_space=pl.ANY)] * 3,
        scratch_shapes=scratch
        + [pltpu.SemaphoreType.DMA((n,)), pltpu.SemaphoreType.DMA((n,)), pltpu.SemaphoreType.DMA((3 * CHUNKS,))],
        compiler_params=pltpu.CompilerParams(collective_id=ident, has_side_effects=True, vmem_limit_bytes=60 * 2**20),
        name=f"gather_{ident}",
    )(*w)


def matmul(a, w):
    return jnp.dot(a, w, preferred_element_type=F32).astype(BF)


def normed(h):
    wide = h.astype(F32)
    scale = lax.rsqrt(jnp.mean(wide**2, -1, keepdims=True) + 1e-6)
    return (wide * scale).astype(BF)


def layer(h, w):
    a = normed(h)
    gate = jnp.dot(a, w[0], preferred_element_type=F32)
    up = jnp.dot(a, w[1], preferred_element_type=F32)
    return h + matmul((jax.nn.silu(gate) * up).astype(BF), w[2])


def solution(mesh):
    def step(x, dy, *arrays):
        weights, ms, vs = arrays[:3], arrays[3:6], arrays[6:]
        x, dy = x[0], dy[0]
        me = lax.axis_index("dp")

        def run(per_layer):
            h = x
            for w in per_layer:
                h = layer(h, w)
            return h

        layers = weights[0].shape[0]
        _, back = jax.vjp(run, [[w[number] for w in weights] for number in range(layers)])
        grads = back(dy)[0]
        rows = (16, 16, 50)
        new = [None] * layers
        full = [None] * layers
        for number in reversed(range(layers)):
            g = [grads[number][i].reshape(s) for i, s in enumerate([(4, 4, 4, 16, FF)] * 2 + [(4, 4, 200, D)])]
            w = [lax.dynamic_slice_in_dim(weights[i][number], me * rows[i], rows[i], 0) for i in range(3)]
            new[number] = scatter_step(g, w, [m[number] for m in ms], [v[number] for v in vs], 2 * number)
            full[number] = gather_step(new[number][0], 2 * number + 1)
        w = [jnp.stack([full[number][i].reshape(weights[i].shape[1:]) for number in range(layers)]) for i in range(3)]
        m, v = ([jnp.stack([new[number][which][i] for number in range(layers)]) for i in range(3)] for which in (1, 2))
        return (*w, *m, *v)

    tokens = P(("rep", "dp"))
    return jax.shard_map(
        step,
        mesh=mesh,
        in_specs=(tokens, tokens) + (P(),) * 3 + (P(None, "dp"),) * 6,
        out_specs=(P("rep"),) * 3 + (P("rep", "dp"),) * 6,
        check_vma=False,
    )
```

time: 2110 us -> 804 us (0.38)
  waiting for transfers between devices: 1010 us -> 0 us
  blocking collectives: 556 us -> 0 us
  Pallas kernels: 0 us -> 333 us
  starting transfers between devices: 39.3 us -> 0 us
  other arithmetic: 69.4 us -> 43.5 us
    unnamed x25 -> x0, waiting for transfers between devices: 748 us -> none
    unnamed x1 -> x0, blocking collectives: 556 us -> none
    pallas_call x0 -> x4, Pallas kernels: none -> 333 us  [the longest x2 175 us: scatter_step(): pl.pallas_call(scatter_kernel, out_shape=[jax.ShapeDtypeStruct(s, t) for...]
    reshape x3 -> x0, waiting for transfers between devices: 265 us -> none  [step(): t.reshape(-1, *t.shape[2:])]
    unnamed x6 -> x5, other arithmetic: 56.5 us -> 0.01 us
    unnamed x60, local copies, waits for them, and re-layouts: 59.8 us -> 16.3 us
    unnamed x18 -> x0, starting transfers between devices: 39.2 us -> none
    another operation x0 -> x9, other arithmetic: none -> 34.2 us  [the longest x3 25.4 us: step(): jnp.stack([full[number][i].reshape(weights[i].shape[1:]) for number in ra...]
  transfers between devices with their start and end apart: 21 -> 0, of which waited for: 6 -> 0; matrix products, arithmetic and copies ran while one was open for 38% -> 0% of each run, Pallas kernels for 0% -> 0%
where the time goes in v1:
time: 804 us; the launch traced here: 794 us
  matrix products  368 us (46%)
  Pallas kernels  333 us (41%)
  local copies, waits for them, and re-layouts  49.3 us (6%)
  other arithmetic  43.5 us (5%)
    pallas_call x2, Pallas kernels, scatter_step(): pl.pallas_call(scatter_kernel, out_shape=[jax.ShapeDtypeStruct(s, t) for...  175 us
    pallas_call x2, Pallas kernels, gather_step(): pl.pallas_call(gather_kernel, out_shape=[jax.ShapeDtypeStruct(s, BF) for...  158 us
    dot_general x5, matrix products, layer(): gate = jnp.dot(a, w[0], preferred_element_type=F32)  130 us
    dot_general x5, matrix products, layer(): up = jnp.dot(a, w[1], preferred_element_type=F32)  127 us
    dot_general x5, matrix products, matmul(): return jnp.dot(a, w, preferred_element_type=F32).astype(BF)  110 us
    another operation x3, other arithmetic, step(): jnp.stack([full[number][i].reshape(weights[i].shape[1:]) for number in ra...  25.4 us
    slice x3, local copies, waits for them, and re-layouts, step(): w[number]  19.3 us
    unnamed x60, local copies, waits for them, and re-layouts  16.3 us

profile of v1, /device:TPU:0, one launch (start us, length us, event | category | flops | bytes accessed | tf_op | source)
XLA Modules:
  0.0 794.4 jit_solution(4311993819426819317)
XLA Ops:
  5.4 2.1 slice_bitcast_fusion.6
  7.5 2.2 slice_bitcast_fusion.4
  9.7 6.5 copy.20
  16.2 3.1 fusion.15
  19.3 6.5 copy.21
  25.8 20.8 %convolution_convert_fusion.1 = bf16[2048,3200]{1,0:T(8,128)(2,1)} fusion(bf16[1,2048,1024]{2,1,0:T(8,128)(2,1)} %param.12, bf16[2,3200,1024]{2,1,0:T(8,128)(2,1)} %param.15), kind=kOutput, calls=%fused_computation.23 | convolution fusion | flops 13428326400 | bytes 23855104 | tf_op jit(solution)/shard_map/transpose(jvp())/dot_general | solution.py:367
  46.6 6.4 fusion.77
  53.7 9.2 %fusion.76 = (bf16[1,1024,3200]{2,1,0:T(8,128)(2,1)S(1)}, bf16[1,1024,3200]{2,1,0:T(8,128)(2,1)}) fusion(bf16[2,1024,3200]{2,1,0:T(8,128)(2,1)} %param.14), kind=kLoop, calls=%fused_computation.111 | loop fusion | bytes 26214400 | tf_op jit(solution)/shard_map/slice | solution.py:396
  62.9 2.2 dynamic-slice_bitcast_fusion.2
  65.2 3.7 fusion.75
  70.6 20.0 %fusion.41 = f32[2048,3200]{1,0:T(8,128)} fusion(bf16[1,2048,1024]{2,1,0:T(8,128)(2,1)} %param.11, f32[2048]{0:T(1024)S(1)} %add_rsqrt_fusion, bf16[2,1024,3200]{2,1,0:T(8,128)(2,1)S(1)} %bitcast.123), kind=kOutput, calls=%fused_computation.63 | convolution fusion | flops 13428064256 | bytes 36970496 | tf_op jit(solution)/shard_map/jvp()/dot_general | solution.py:378
  90.6 32.3 %multiply_convert_fusion.1 = (bf16[2048,3200]{1,0:T(8,128)(2,1)}, f32[2048,3200]{1,0:T(8,128)}) fusion(f32[2048,3200]{1,0:T(8,128)} %fusion.41, bf16[2,1024,3200]{2,1,0:T(8,128)(2,1)} %param.14, bf16[1,2048,1024]{2,1,0:T(8,128)(2,1)} %param.11, f32[2048]{0:T(1024)S(1)} %add_rsqrt_fusion), kind=kOutput, calls=%fused_computation.17 | convolution fusion | flops 13467385856 | bytes 76292096 | tf_op jit(solution)/shard_map/jvp()/dot_general | solution.py:379
  122.9 21.9 %fusion.19 = (f32[2048]{0:T(1024)S(1)}, bf16[2048,1024]{0,1:T(8,128)(2,1)}) fusion(bf16[2048,3200]{1,0:T(8,128)(2,1)} %get-tuple-element.84, bf16[2,3200,1024]{2,1,0:T(8,128)(2,1)} %param.15, bf16[1,2048,1024]{1,2,0:T(8,128)(2,1)} %copy.20), kind=kOutput, calls=%fused_computation.40 | convolution fusion | flops 13432256512 | bytes 28057600 | tf_op jit(solution)/shard_map/jvp()/dot_general | solution.py:367
  144.8 23.3 %fusion.28 = f32[2048,3200]{1,0:T(8,128)} fusion(bf16[2048,1024]{0,1:T(8,128)(2,1)} %get-tuple-element.87, f32[2048]{0:T(1024)S(1)} %fusion.60, bf16[2,1024,3200]{2,1,0:T(8,128)(2,1)} %param.14), kind=kOutput, calls=%fused_computation.50 | convolution fusion | flops 13428064256 | bytes 36970496 | tf_op jit(solution)/shard_map/jvp()/dot_general | solution.py:379
  168.1 38.7 %fusion.2 = (bf16[2048,3200]{1,0:T(8,128)(2,1)}, f32[2048,3200]{1,0:T(8,128)}) fusion(f32[2048,3200]{1,0:T(8,128)} %fusion.28, bf16[2048,3200]{1,0:T(8,128)(2,1)} %convolution_convert_fusion.1, bf16[2,1024,3200]{2,1,0:T(8,128)(2,1)} %param.13, bf16[2048,1024]{0,1:T(8,128)(2,1)} %get-tuple-element.87, f32[2048]{0:T(1024)S(1)} %fusion.60), kind=kOutput, calls=%fused_computation.8 | convolution fusion | flops 13506707456 | bytes 89399296 | tf_op jit(solution)/shard_map/jvp()/dot_general | solution.py:378
  206.8 25.7 %fusion.25 = bf16[3200,1024]{1,0:T(8,128)(2,1)} fusion(f32[2048,3200]{1,0:T(8,128)} %fusion.28, bf16[1,2048,1024]{2,1,0:T(8,128)(2,1)} %param.12, f32[2048,3200]{1,0:T(8,128)} %get-tuple-element.89), kind=kOutput, calls=%fused_computation.45 | convolution fusion | flops 13464371200 | bytes 63176704 | tf_op jit(solution)/shard_map/transpose(jvp())/dot_general | solution.py:367
  232.5 22.8 %fusion.12 = bf16[2048,1024]{0,1:T(8,128)(2,1)} fusion(bf16[2048,3200]{1,0:T(8,128)(2,1)} %convolution_convert_fusion.1, bf16[2,1024,3200]{2,1,0:T(8,128)(2,1)} %param.14, f32[2048,3200]{1,0:T(8,128)} %get-tuple-element.89), kind=kOutput, calls=%fused_computation.21 | convolution fusion | flops 13461094400 | bytes 50069504 | tf_op jit(solution)/shard_map/transpose(jvp())/dot_general | solution.py:379
  255.3 24.1 %fusion.26 = bf16[1024,3200]{1,0:T(8,128)(2,1)} fusion(bf16[2048,3200]{1,0:T(8,128)(2,1)} %convolution_convert_fusion.1, bf16[2048,1024]{0,1:T(8,128)(2,1)S(1)} %copy-done.2, f32[2048]{0:T(1024)S(1)} %fusion.60, f32[2048,3200]{1,0:T(8,128)} %get-tuple-element.89), kind=kOutput, calls=%fused_computation.46 | convolution fusion | flops 13470662656 | bytes 50077696 | tf_op jit(solution)/shard_map/transpose(jvp())/dot_general | solution.py:379
  279.5 21.9 %fusion.21 = (f32[2048]{0:T(1024)S(1)}, bf16[2048,1024]{0,1:T(8,128)(2,1)}) fusion(bf16[2048,1024]{0,1:T(8,128)(2,1)S(1)} %copy-done.2, bf16[2048,1024]{0,1:T(8,128)(2,1)} %fusion.12, bf16[2048,3200]{1,0:T(8,128)(2,1)} %get-tuple-element.88, bf16[2,1024,3200]{2,1,0:T(8,128)(2,1)} %param.13), kind=kOutput, calls=%fused_computation.42 | convolution fusion | flops 13432256512 | bytes 32251904 | tf_op jit(solution)/shard_map/transpose(jvp())/dot_general | solution.py:378
  301.4 20.1 %convolution_convert_fusion.3 = bf16[1024,3200]{1,0:T(8,128)(2,1)} fusion(bf16[2048,3200]{1,0:T(8,128)(2,1)} %get-tuple-element.88, bf16[2048,1024]{0,1:T(8,128)(2,1)S(1)} %copy-done.2, f32[2048]{0:T(1024)S(1)} %fusion.60), kind=kOutput, calls=%fused_computation.49 | convolution fusion | flops 13428064256 | bytes 23863296 | tf_op jit(solution)/shard_map/transpose(jvp())/dot_general | solution.py:378
  321.5 90.2 %scatter_2.1 = (bf16[16,3200]{1,0:T(8,128)(2,1)}, bf16[16,3200]{1,0:T(8,128)(2,1)}, bf16[50,1024]{1,0:T(8,128)(2,1)}, f32[16,3200]{1,0:T(8,128)}, f32[16,3200]{1...) custom-call(bf16[4,4,4,16,3200]{4,3,2,1,0:T(8,128)(2,1)} %bitcast.131, ...), custom_call_target="tpu_custom_call" | custom-call | tf_op jit(solution)/shard_map/scatter_2/pallas_call | solution.py:308
  411.7 6.2 fusion.45
  418.0 20.8 %convolution_convert_fusion.2 = bf16[3200,1024]{1,0:T(8,128)(2,1)} fusion(bf16[2048,3200]{1,0:T(8,128)(2,1)} %get-tuple-element.84, bf16[2048,1024]{0,1:T(8,128)(2,1)S(1)} %fusion.45), kind=kOutput, calls=%fused_computation.48 | convolution fusion | flops 13425049600 | bytes 23855104 | tf_op jit(solution)/shard_map/transpose(jvp())/dot_general | solution.py:367
  438.8 21.2 %convolution_convert_fusion = bf16[2048,3200]{1,0:T(8,128)(2,1)} fusion(bf16[2048,1024]{0,1:T(8,128)(2,1)} %copy-done.3, bf16[2,3200,1024]{2,1,0:T(8,128)(2,1)} %param.15), kind=kOutput, calls=%fused_computation.22 | convolution fusion | flops 13428326400 | bytes 23855104 | tf_op jit(solution)/shard_map/transpose(jvp())/dot_general | solution.py:367
  460.0 29.6 %fusion.22 = bf16[1024,3200]{1,0:T(8,128)(2,1)} fusion(f32[2048,3200]{1,0:T(8,128)} %fusion.41, f32[2048,3200]{1,0:T(8,128)} %get-tuple-element.85, bf16[2048,3200]{1,0:T(8,128)(2,1)} %convolution_convert_fusion, bf16[1,2048,1024]{1,2,0:T(8,128)(2,1)S(1)} %copy-done, f32[2048]{0:T(1024)S(1)} %copy-done.13), kind=kOutput, calls=%fused_computation.44 | convolution fusion | flops 13503430656 | bytes 76292096 | tf_op jit(solution)/shard_map/transpose(jvp())/dot_general | solution.py:378
  489.6 24.2 %fusion.27 = bf16[1024,3200]{1,0:T(8,128)(2,1)} fusion(bf16[2048,3200]{1,0:T(8,128)(2,1)} %convolution_convert_fusion, f32[2048,3200]{1,0:T(8,128)} %fusion.41, bf16[1,2048,1024]{1,2,0:T(8,128)(2,1)S(1)} %copy-done, f32[2048]{0:T(1024)S(1)} %copy-done.13), kind=kOutput, calls=%fused_computation.47 | convolution fusion | flops 13470662656 | bytes 50077696 | tf_op jit(solution)/shard_map/transpose(jvp())/dot_general | solution.py:379
  513.9 85.0 %scatter_0.1 = (bf16[16,3200]{1,0:T(8,128)(2,1)}, bf16[16,3200]{1,0:T(8,128)(2,1)}, bf16[50,1024]{1,0:T(8,128)(2,1)}, f32[16,3200]{1,0:T(8,128)}, f32[16,3200]{1...) custom-call(bf16[4,4,4,16,3200]{4,3,2,1,0:T(8,128)(2,1)} %bitcast.129, ...), custom_call_target="tpu_custom_call" | custom-call | tf_op jit(solution)/shard_map/scatter_0/pallas_call | solution.py:308
  609.8 79.3 %gather_1.1 = (bf16[4,4,4,16,3200]{4,3,2,1,0:T(8,128)(2,1)}, bf16[4,4,4,16,3200]{4,3,2,1,0:T(8,128)(2,1)}, bf16[4,4,200,1024]{3,2,1,0:T(8,128)(2,1)}) custom-call(bf16[16,3200]{1,0:T(8,128)(2,1)} %get-tuple-element.33.refs_0_, bf16[16,3200]{1,0:T(8,128)(2,1)} %get-tuple-element.34.refs_1_, bf16[50,1024]{1,0:T(8,128)(2,1)} %get-tuple-element.35.refs_2_), custom_call_target="tpu_custom_call" | custom-call | tf_op jit(solution)/shard_map/gather_1/pallas_call | solution.py:354
  689.2 78.5 %gather_3.1 = (bf16[4,4,4,16,3200]{4,3,2,1,0:T(8,128)(2,1)}, bf16[4,4,4,16,3200]{4,3,2,1,0:T(8,128)(2,1)}, bf16[4,4,200,1024]{3,2,1,0:T(8,128)(2,1)}) custom-call(bf16[16,3200]{1,0:T(8,128)(2,1)} %get-tuple-element.37.refs_0_, bf16[16,3200]{1,0:T(8,128)(2,1)} %get-tuple-element.38.refs_1_, bf16[50,1024]{1,0:T(8,128)(2,1)} %get-tuple-element.39.refs_2_), custom_call_target="tpu_custom_call" | custom-call | tf_op jit(solution)/shard_map/gather_3/pallas_call | solution.py:354
  767.7 12.7 %pad_maximum_fusion = bf16[2,1024,3200]{2,1,0:T(8,128)(2,1)} fusion(bf16[1,1024,3200]{2,1,0:T(8,128)(2,1)} %bitcast.143, bf16[1,1024,3200]{2,1,0:T(8,128)(2,1)} %bitcast.138), kind=kLoop, calls=%fused_computation.29 | loop fusion | flops 6553600 | bytes 26214400 | tf_op jit(solution)/shard_map/stack | solution.py:406
  780.5 7.4 pad_maximum_fusion.1
  788.9 5.3 pad_maximum_fusion.2
  (78 shorter events, 19.2 us)
Async XLA Ops:
  19.3 71.3 %copy-start.12 = (f32[2048]{0:T(1024)}, f32[2048]{0:T(1024)S(1)}, u32[]{:S(2)}) copy-start(f32[2048]{0:T(1024)S(1)} %add_rsqrt_fusion) | copy-start | bytes 24580
  46.6 18.6 %slice-start.4 = ((s8[13107200]{0:T(1024)(128)(4,1)}), s8[4194304]{0:T(1024)(128)(4,1)S(1)}, s32[]{:S(2)}) async-start(s8[13107200]{0:T(1024)(128)(4,1)} %bitcast.124), calls=%async_computation.4 | async-start | bytes 8388608
  46.6 18.6 %slice-start.5 = ((s8[13107200]{0:T(1024)(128)(4,1)}), s8[4194304]{0:T(1024)(128)(4,1)S(1)}, s32[]{:S(2)}) async-start(s8[13107200]{0:T(1024)(128)(4,1)} %bitcast.124), calls=%async_computation.5 | async-start | bytes 8388608
  53.7 11.5 %slice-start.6 = ((s8[13107200]{0:T(1024)(128)(4,1)}), s8[4194304]{0:T(1024)(128)(4,1)S(1)}, s32[]{:S(2)}) async-start(s8[13107200]{0:T(1024)(128)(4,1)} %bitcast.124), calls=%async_computation.6 | async-start | bytes 8388608
  53.7 11.5 %slice-start.7 = ((s8[13107200]{0:T(1024)(128)(4,1)}), s8[524288]{0:T(1024)(128)(4,1)S(1)}, s32[]{:S(2)}) async-start(s8[13107200]{0:T(1024)(128)(4,1)} %bitcast.124), calls=%async_computation.7 | async-start | bytes 1048576
  53.7 16.9 %slice-start = ((s8[13107200]{0:T(1024)(128)(4,1)}), s8[4194304]{0:T(1024)(128)(4,1)S(1)}, s32[]{:S(2)}) async-start(s8[13107200]{0:T(1024)(128)(4,1)} %bitcast.122), calls=%async_computation | async-start | bytes 8388608
  53.7 16.9 %slice-start.1 = ((s8[13107200]{0:T(1024)(128)(4,1)}), s8[4194304]{0:T(1024)(128)(4,1)S(1)}, s32[]{:S(2)}) async-start(s8[13107200]{0:T(1024)(128)(4,1)} %bitcast.122), calls=%async_computation.1 | async-start | bytes 8388608
  65.2 5.4 slice-start.2
  65.2 5.4 slice-start.3
  144.8 23.3 %copy-start.10 = (f32[2048]{0:T(1024)}, f32[2048]{0:T(1024)S(1)}, u32[]{:S(2)}) copy-start(f32[2048]{0:T(1024)S(1)} %get-tuple-element.86) | copy-start | bytes 24580
  232.5 22.8 %copy-start.2 = (bf16[2048,1024]{0,1:T(8,128)(2,1)S(1)}, bf16[2048,1024]{0,1:T(8,128)(2,1)}, u32[]{:S(2)}) copy-start(bf16[2048,1024]{0,1:T(8,128)(2,1)} %get-tuple-element.87) | copy-start | bytes 12582916
  321.5 90.2 %copy-start.11 = (f32[2048]{0:T(1024)S(1)}, f32[2048]{0:T(1024)}, u32[]{:S(2)}) copy-start(f32[2048]{0:T(1024)} %copy-done.10) | copy-start | bytes 24580
  418.0 20.8 %copy-start.3 = (bf16[2048,1024]{0,1:T(8,128)(2,1)}, bf16[2048,1024]{0,1:T(8,128)(2,1)S(1)}, u32[]{:S(2)}) copy-start(bf16[2048,1024]{0,1:T(8,128)(2,1)S(1)} %fusion.45) | copy-start | bytes 12582916
  438.8 21.2 %copy-start = (bf16[1,2048,1024]{1,2,0:T(8,128)(2,1)S(1)}, bf16[1,2048,1024]{1,2,0:T(8,128)(2,1)}, u32[]{:S(2)}) copy-start(bf16[1,2048,1024]{1,2,0:T(8,128)(2,1)} %copy.20) | copy-start | bytes 12582916
  438.8 21.2 %copy-start.13 = (f32[2048]{0:T(1024)S(1)}, f32[2048]{0:T(1024)}, u32[]{:S(2)}) copy-start(f32[2048]{0:T(1024)} %copy-done.12) | copy-start | bytes 24580
  513.9 85.0 %copy-start.9 = (f32[16,3200]{1,0:T(8,128)S(1)}, f32[16,3200]{1,0:T(8,128)}, u32[]{:S(2)}) copy-start(f32[16,3200]{1,0:T(8,128)} %get-tuple-element.46) | copy-start | bytes 614404
  513.9 86.7 %copy-start.8 = (f32[16,3200]{1,0:T(8,128)S(1)}, f32[16,3200]{1,0:T(8,128)}, u32[]{:S(2)}) copy-start(f32[16,3200]{1,0:T(8,128)} %get-tuple-element.48) | copy-start | bytes 614404
  513.9 88.4 %copy-start.7 = (f32[16,3200]{1,0:T(8,128)S(1)}, f32[16,3200]{1,0:T(8,128)}, u32[]{:S(2)}) copy-start(f32[16,3200]{1,0:T(8,128)} %get-tuple-element.52) | copy-start | bytes 614404
  513.9 90.1 %copy-start.6 = (f32[16,3200]{1,0:T(8,128)S(1)}, f32[16,3200]{1,0:T(8,128)}, u32[]{:S(2)}) copy-start(f32[16,3200]{1,0:T(8,128)} %get-tuple-element.54) | copy-start | bytes 614404
  513.9 91.8 %copy-start.5 = (f32[50,1024]{1,0:T(8,128)S(1)}, f32[50,1024]{1,0:T(8,128)}, u32[]{:S(2)}) copy-start(f32[50,1024]{1,0:T(8,128)} %get-tuple-element.50) | copy-start | bytes 614404
  513.9 93.9 %copy-start.4 = (f32[50,1024]{1,0:T(8,128)S(1)}, f32[50,1024]{1,0:T(8,128)}, u32[]{:S(2)}) copy-start(f32[50,1024]{1,0:T(8,128)} %get-tuple-element.56) | copy-start | bytes 614404
  689.1 91.3 %slice-start.10 = ((s8[6553600]{0:T(1024)(128)(4,1)}), s8[2359296]{0:T(1024)(128)(4,1)S(1)}, s32[]{:S(2)}) async-start(s8[6553600]{0:T(1024)(128)(4,1)} %bitcast.135), calls=%async_computation.10 | async-start | bytes 4718592
  767.7 12.8 %slice-start.11 = ((s8[6553600]{0:T(1024)(128)(4,1)}), s8[4194304]{0:T(1024)(128)(4,1)S(1)}, s32[]{:S(2)}) async-start(s8[6553600]{0:T(1024)(128)(4,1)} %bitcast.135), calls=%async_computation.11 | async-start | bytes 8388608
  767.7 12.8 %copy-start.1 = (bf16[4,4,4,16,3200]{4,3,2,1,0:T(8,128)(2,1)S(1)}, bf16[4,4,4,16,3200]{4,3,2,1,0:T(8,128)(2,1)}, u32[]{:S(2)}) copy-start(bf16[4,4,4,16,3200]{4,3,2,1,0:T(8,128)(2,1)} %get-tuple-element.42) | copy-start | bytes 19660804
  767.7 20.1 %slice-start.8 = ((s8[6553600]{0:T(1024)(128)(4,1)}), s8[4194304]{0:T(1024)(128)(4,1)S(1)}, s32[]{:S(2)}) async-start(s8[6553600]{0:T(1024)(128)(4,1)} %bitcast.132), calls=%async_computation.8 | async-start | bytes 8388608
  767.7 20.1 %slice-start.12 = ((s8[6553600]{0:T(1024)(128)(4,1)}), s8[4194304]{0:T(1024)(128)(4,1)S(1)}, s32[]{:S(2)}) async-start(s8[6553600]{0:T(1024)(128)(4,1)} %bitcast.139), calls=%async_computation.12 | async-start | bytes 8388608
  780.4 7.4 slice-start.9
  780.4 8.5 %slice-start.13 = ((s8[6553600]{0:T(1024)(128)(4,1)}), s8[2359296]{0:T(1024)(128)(4,1)S(1)}, s32[]{:S(2)}) async-start(s8[6553600]{0:T(1024)(128)(4,1)} %bitcast.139), calls=%async_computation.13 | async-start | bytes 4718592
